TPU v7x, 32 devices: a whole 2x2x4 slice. The times are simulated.
32 devices in a mesh: wide: 8 (over y, x, core), narrow: 4 (over z).
Axes of the slice: x: 2, y: 2, z: 4, core: 2. Of those that a mesh axis runs over, the one named last changes fastest.
Arguments:
- tokens: bfloat16 [65536, 768], P(('wide', 'narrow')), may hold values from -6 to 6
- cotangent: bfloat16 [65536, 768], P(('wide', 'narrow')), may hold values from -6 to 6
- lengths: int32 [64, 24], P(('wide', 'narrow')), may hold values from 1 to 128, 1024 in all within a row
- features: float32 [64, 384], replicated, may hold values from -5 to 5
- ln1_gain: bfloat16 [768], P('wide'), may hold values from 0.5 to 1.5
- ln1_bias: bfloat16 [768], P('wide'), may hold values from -1.75 to 1.75
- q_weight: bfloat16 [768, 768], P('wide'), may hold values from -0.21875 to 0.21875
- q_bias: bfloat16 [768], P('wide'), may hold values from -3 to 3
- k_weight: bfloat16 [768, 768], P('wide'), may hold values from -0.21875 to 0.21875
- k_bias: bfloat16 [768], P('wide'), may hold values from -3 to 3
- v_weight: bfloat16 [768, 768], P('wide'), may hold values from -0.21875 to 0.21875
- v_bias: bfloat16 [768], P('wide'), may hold values from -3 to 3
- out_weight: bfloat16 [768, 768], P('wide'), may hold values from -0.875 to 0.875
- out_bias: bfloat16 [768], P('wide'), may hold values from -3 to 3
- ln2_gain: bfloat16 [768], P('wide'), may hold values from 0.5 to 1.5
- ln2_bias: bfloat16 [768], P('wide'), may hold values from -1.75 to 1.75
- up_weight: bfloat16 [768, 3072], P('wide'), may hold values from -0.21875 to 0.21875
- up_bias: bfloat16 [3072], P('wide'), may hold values from -3 to 3
- down_weight: bfloat16 [3072, 768], P('wide'), may hold values from -0.109375 to 0.109375
- down_bias: bfloat16 [768], P('wide'), may hold values from -3 to 3
Outputs:
- output: bfloat16 [65536, 768], P(('wide', 'narrow'))
- input_grad: float32 [65536, 768], P(('wide', 'narrow'))
- ln1_gain_grad: float32 [768], P('wide')
- ln1_bias_grad: float32 [768], P('wide')
- q_weight_grad: float32 [768, 768], P('wide')
- q_bias_grad: float32 [768], P('wide')
- k_weight_grad: float32 [768, 768], P('wide')
- k_bias_grad: float32 [768], P('wide')
- v_weight_grad: float32 [768, 768], P('wide')
- v_bias_grad: float32 [768], P('wide')
- out_weight_grad: float32 [768, 768], P('wide')
- out_bias_grad: float32 [768], P('wide')
- ln2_gain_grad: float32 [768], P('wide')
- ln2_bias_grad: float32 [768], P('wide')
- up_weight_grad: float32 [768, 3072], P('wide')
- up_bias_grad: float32 [3072], P('wide')
- down_weight_grad: float32 [3072, 768], P('wide')
- down_bias_grad: float32 [768], P('wide')
Inputs may be any that keep to these rules, and one draw needn't show every extreme that they name: Each row holds the 24 piece lengths of one sequence in order, summing to 1024; the largest is exactly 128.
All inputs are finite; a program needn't handle non-finite values.
Results may differ from a plain program's by a relative error of at most 0.03.
Values may be sent and summed in bfloat16 or wider, within the bound.
A program may use at most 192 MiB of HBM per device.

v0:
```python
from functools import partial
import math
import jax
import jax.numpy as jnp
from jax import lax
from jax.sharding import PartitionSpec as P

D = 768
HEADS = 12
HD = 64
FEAT = 32
SEGS = 24
EPSILON = 1e-05
HIGHEST = lax.Precision.HIGHEST


def pieces(lens_row, seq_len):
    seg_end = jnp.cumsum(lens_row)
    seg_start = seg_end - lens_row
    places = jnp.arange(seq_len, dtype=jnp.int32)
    segment = jnp.sum((places[:, None] >= seg_end[None, :]).astype(jnp.int32), axis=1)
    slots = jnp.arange(SEGS, dtype=jnp.int32)
    begins = jnp.sum(jnp.where(segment[:, None] == slots[None, :], seg_start[None, :], 0), axis=1)
    position = places - begins
    valid = (segment < SEGS - 1).astype(jnp.float32)
    allowed = (places[None, :] <= places[:, None]) & (segment[None, :] == segment[:, None])
    return (position, valid, allowed)


def rotate(heads_field, position):
    half = HD // 2
    rates = jnp.exp(jnp.arange(half, dtype=jnp.float32) * (-2.0 * math.log(10000.0) / HD))
    angles = position.astype(jnp.float32)[:, None] * rates[None, :]
    cosine = jnp.cos(angles)[:, None, :]
    sine = jnp.sin(angles)[:, None, :]
    first = heads_field[..., :half]
    second = heads_field[..., half:]
    return jnp.concatenate(
        [first * cosine - second * sine, second * cosine + first * sine], axis=-1
    )


def featurize(rotated, features):
    table = features.reshape(HD, HEADS, FEAT)
    scores = jnp.einsum("lhe,ehm->lhm", rotated, table, precision=HIGHEST) * 0.125
    return jax.nn.elu(scores) + 1.0


def normalize(stream, gain, shift):
    average = jnp.mean(stream, axis=-1, keepdims=True)
    centered = stream - average
    variance = jnp.mean(centered * centered, axis=-1, keepdims=True)
    return centered * lax.rsqrt(variance + EPSILON) * gain + shift


def contract_rows(left, right):
    return lax.dot_general(
        left, right, (((0,), (0,)), ((), ())), preferred_element_type=jnp.float32
    )


def times_transposed(left, right):
    return lax.dot_general(
        left, right, (((1,), (1,)), ((), ())), preferred_element_type=jnp.float32
    )


def column_sums(matrix):
    return jnp.sum(matrix.astype(jnp.float32), axis=0)


def collect(shards):
    return (
        lax.all_gather(shards[0], "wide", axis=0, tiled=True),
        lax.all_gather(shards[1], "wide", axis=0, tiled=True),
        lax.all_gather(shards[2], "wide", axis=0, tiled=True),
        lax.all_gather(shards[3], "wide", axis=0, tiled=True),
        lax.all_gather(shards[4], "wide", axis=0, tiled=True),
        lax.all_gather(shards[5], "wide", axis=0, tiled=True),
        lax.all_gather(shards[6], "wide", axis=0, tiled=True),
        lax.all_gather(shards[7], "wide", axis=0, tiled=True),
        lax.all_gather(shards[8], "wide", axis=0, tiled=True),
        lax.all_gather(shards[9], "wide", axis=0, tiled=True),
        lax.all_gather(shards[10], "wide", axis=0, tiled=True),
        lax.all_gather(shards[11], "wide", axis=0, tiled=True),
        lax.all_gather(shards[12], "wide", axis=0, tiled=True),
        lax.all_gather(shards[13], "wide", axis=0, tiled=True),
        lax.all_gather(shards[14], "wide", axis=0, tiled=True),
        lax.all_gather(shards[15], "wide", axis=0, tiled=True),
    )


def settle(grads):
    shares = (
        lax.psum_scatter(grads[0], "wide", scatter_dimension=0, tiled=True),
        lax.psum_scatter(grads[1], "wide", scatter_dimension=0, tiled=True),
        lax.psum_scatter(grads[2], "wide", scatter_dimension=0, tiled=True),
        lax.psum_scatter(grads[3], "wide", scatter_dimension=0, tiled=True),
        lax.psum_scatter(grads[4], "wide", scatter_dimension=0, tiled=True),
        lax.psum_scatter(grads[5], "wide", scatter_dimension=0, tiled=True),
        lax.psum_scatter(grads[6], "wide", scatter_dimension=0, tiled=True),
        lax.psum_scatter(grads[7], "wide", scatter_dimension=0, tiled=True),
        lax.psum_scatter(grads[8], "wide", scatter_dimension=0, tiled=True),
        lax.psum_scatter(grads[9], "wide", scatter_dimension=0, tiled=True),
        lax.psum_scatter(grads[10], "wide", scatter_dimension=0, tiled=True),
        lax.psum_scatter(grads[11], "wide", scatter_dimension=0, tiled=True),
        lax.psum_scatter(grads[12], "wide", scatter_dimension=0, tiled=True),
        lax.psum_scatter(grads[13], "wide", scatter_dimension=0, tiled=True),
        lax.psum_scatter(grads[14], "wide", scatter_dimension=0, tiled=True),
        lax.psum_scatter(grads[15], "wide", scatter_dimension=0, tiled=True),
    )
    return (
        lax.psum(shares[0].astype(jnp.bfloat16), "narrow").astype(jnp.float32),
        lax.psum(shares[1].astype(jnp.bfloat16), "narrow").astype(jnp.float32),
        lax.psum(shares[2].astype(jnp.bfloat16), "narrow").astype(jnp.float32),
        lax.psum(shares[3].astype(jnp.bfloat16), "narrow").astype(jnp.float32),
        lax.psum(shares[4].astype(jnp.bfloat16), "narrow").astype(jnp.float32),
        lax.psum(shares[5].astype(jnp.bfloat16), "narrow").astype(jnp.float32),
        lax.psum(shares[6].astype(jnp.bfloat16), "narrow").astype(jnp.float32),
        lax.psum(shares[7].astype(jnp.bfloat16), "narrow").astype(jnp.float32),
        lax.psum(shares[8].astype(jnp.bfloat16), "narrow").astype(jnp.float32),
        lax.psum(shares[9].astype(jnp.bfloat16), "narrow").astype(jnp.float32),
        lax.psum(shares[10].astype(jnp.bfloat16), "narrow").astype(jnp.float32),
        lax.psum(shares[11].astype(jnp.bfloat16), "narrow").astype(jnp.float32),
        lax.psum(shares[12].astype(jnp.bfloat16), "narrow").astype(jnp.float32),
        lax.psum(shares[13].astype(jnp.bfloat16), "narrow").astype(jnp.float32),
        lax.psum(shares[14].astype(jnp.bfloat16), "narrow").astype(jnp.float32),
        lax.psum(shares[15].astype(jnp.bfloat16), "narrow").astype(jnp.float32),
    )


def head_forward(operands, allowed):
    query_feat, key_feat, head_value = operands
    scores = jnp.where(allowed, times_transposed(query_feat, key_feat), 0.0)
    denominator = jnp.sum(scores, axis=1)
    numerator = jnp.dot(scores.astype(jnp.bfloat16), head_value, preferred_element_type=jnp.float32)
    return (numerator, denominator)


def head_backward(operands, allowed, valid):
    query_feat, key_feat, head_value, numerator, denominator, head_grad = operands
    scores = jnp.where(allowed, times_transposed(query_feat, key_feat), 0.0)
    scores_low = scores.astype(jnp.bfloat16)
    scaled = head_grad * valid[:, None]
    grad_num = (scaled / denominator[:, None]).astype(jnp.bfloat16)
    grad_den = -jnp.sum(scaled * numerator, axis=1) / (denominator * denominator)
    grad_scores = (times_transposed(grad_num, head_value) + grad_den[:, None]).astype(jnp.bfloat16)
    grad_scores = jnp.where(allowed, grad_scores, jnp.zeros((), jnp.bfloat16))
    grad_value = contract_rows(scores_low, grad_num)
    grad_query = jnp.dot(grad_scores, key_feat, preferred_element_type=jnp.float32)
    grad_key = contract_rows(grad_scores, query_feat)
    return (grad_query, grad_key, grad_value)


def run_layer(weights, shards, rows, upward, lens_row, features):
    (
        gain_first,
        shift_first,
        query_mat,
        query_add,
        key_mat,
        key_add,
        value_mat,
        value_add,
        proj_mat,
        proj_add,
        gain_second,
        shift_second,
        up_mat,
        up_add,
        down_mat,
        down_add,
    ) = weights
    seq_len = rows.shape[0]
    stream = rows.astype(jnp.float32)
    position, valid, allowed = pieces(lens_row, seq_len)
    normed_one, norm_one_back = jax.vjp(
        normalize, stream, gain_first.astype(jnp.float32), shift_first.astype(jnp.float32)
    )
    hidden_one = normed_one.astype(jnp.bfloat16)
    query_pre = jnp.dot(
        hidden_one, query_mat, preferred_element_type=jnp.float32
    ) + query_add.astype(jnp.float32)
    key_pre = jnp.dot(hidden_one, key_mat, preferred_element_type=jnp.float32) + key_add.astype(
        jnp.float32
    )
    values = (
        jnp.dot(hidden_one, value_mat, preferred_element_type=jnp.float32)
        + value_add.astype(jnp.float32)
    ).astype(jnp.bfloat16)

    def features_of(projected):
        return featurize(rotate(projected.reshape(seq_len, HEADS, HD), position), features)

    query_feat_full, query_back = jax.vjp(features_of, query_pre)
    key_feat_full, key_back = jax.vjp(features_of, key_pre)
    heads_query = jnp.transpose(query_feat_full.astype(jnp.bfloat16), (1, 0, 2))
    heads_key = jnp.transpose(key_feat_full.astype(jnp.bfloat16), (1, 0, 2))
    heads_value = jnp.transpose(values.reshape(seq_len, HEADS, HD), (1, 0, 2))
    numerator, denominator = lax.map(
        partial(head_forward, allowed=allowed), (heads_query, heads_key, heads_value)
    )
    mixed = numerator / denominator[:, :, None] * valid[None, :, None]
    attended = jnp.transpose(mixed, (1, 0, 2)).reshape(seq_len, D).astype(jnp.bfloat16)
    residual = stream + (
        jnp.dot(attended, proj_mat, preferred_element_type=jnp.float32)
        + proj_add.astype(jnp.float32)
    )
    normed_two, norm_two_back = jax.vjp(
        normalize, residual, gain_second.astype(jnp.float32), shift_second.astype(jnp.float32)
    )
    hidden_two = normed_two.astype(jnp.bfloat16)
    upper = jnp.dot(hidden_two, up_mat, preferred_element_type=jnp.float32) + up_add.astype(
        jnp.float32
    )
    activated, gelu_back = jax.vjp(partial(jax.nn.gelu, approximate=False), upper)
    act_low = activated.astype(jnp.bfloat16)
    result = residual + (
        jnp.dot(act_low, down_mat, preferred_element_type=jnp.float32)
        + down_add.astype(jnp.float32)
    )
    output = result.astype(jnp.bfloat16)
    anchored = lax.optimization_barrier((shards, result))
    again = collect(anchored[0])
    query_mat, key_mat, value_mat, proj_mat, up_mat, down_mat = (
        again[2],
        again[4],
        again[6],
        again[8],
        again[12],
        again[14],
    )
    grad_out = upward.astype(jnp.float32)
    down_grad = contract_rows(act_low, upward)
    down_bias_grad = column_sums(upward)
    grad_act = times_transposed(upward, down_mat)
    grad_upper = gelu_back(grad_act)[0].astype(jnp.bfloat16)
    up_grad = contract_rows(hidden_two, grad_upper)
    up_bias_grad = column_sums(grad_upper)
    grad_hidden_two = times_transposed(grad_upper, up_mat)
    grad_residual_norm, gain_two_grad, shift_two_grad = norm_two_back(grad_hidden_two)
    grad_residual = grad_out + grad_residual_norm
    grad_proj_in = grad_residual.astype(jnp.bfloat16)
    proj_grad = contract_rows(attended, grad_proj_in)
    proj_bias_grad = column_sums(grad_proj_in)
    grad_attended = times_transposed(grad_proj_in, proj_mat)
    heads_grad = jnp.transpose(grad_attended.reshape(seq_len, HEADS, HD), (1, 0, 2))
    grad_qfeat, grad_kfeat, grad_vheads = lax.map(
        partial(head_backward, allowed=allowed, valid=valid),
        (heads_query, heads_key, heads_value, numerator, denominator, heads_grad),
    )
    grad_query = query_back(jnp.transpose(grad_qfeat, (1, 0, 2)))[0].astype(jnp.bfloat16)
    grad_key = key_back(jnp.transpose(grad_kfeat, (1, 0, 2)))[0].astype(jnp.bfloat16)
    grad_value = jnp.transpose(grad_vheads, (1, 0, 2)).reshape(seq_len, D).astype(jnp.bfloat16)
    query_grad = contract_rows(hidden_one, grad_query)
    query_bias_grad = column_sums(grad_query)
    key_grad = contract_rows(hidden_one, grad_key)
    key_bias_grad = column_sums(grad_key)
    value_grad = contract_rows(hidden_one, grad_value)
    value_bias_grad = column_sums(grad_value)
    grad_hidden_one = (
        times_transposed(grad_query, query_mat)
        + times_transposed(grad_key, key_mat)
        + times_transposed(grad_value, value_mat)
    )
    grad_stream_norm, gain_one_grad, shift_one_grad = norm_one_back(grad_hidden_one)
    input_grad = grad_residual + grad_stream_norm
    grads = (
        gain_one_grad,
        shift_one_grad,
        query_grad,
        query_bias_grad,
        key_grad,
        key_bias_grad,
        value_grad,
        value_bias_grad,
        proj_grad,
        proj_bias_grad,
        gain_two_grad,
        shift_two_grad,
        up_grad,
        up_bias_grad,
        down_grad,
        down_bias_grad,
    )
    return ((output, input_grad), grads)


def on_device(
    tokens,
    cotangent,
    lengths,
    features,
    ln1_gain,
    ln1_bias,
    q_weight,
    q_bias,
    k_weight,
    k_bias,
    v_weight,
    v_bias,
    out_weight,
    out_bias,
    ln2_gain,
    ln2_bias,
    up_weight,
    up_bias,
    down_weight,
    down_bias,
):
    shards = (
        ln1_gain,
        ln1_bias,
        q_weight,
        q_bias,
        k_weight,
        k_bias,
        v_weight,
        v_bias,
        out_weight,
        out_bias,
        ln2_gain,
        ln2_bias,
        up_weight,
        up_bias,
        down_weight,
        down_bias,
    )
    micro_count = lengths.shape[0]
    seq_len = tokens.shape[0] // micro_count
    stream = tokens.reshape(micro_count, seq_len, D)
    upstream = cotangent.reshape(micro_count, seq_len, D)

    def process(totals, operands):
        rows, upward, lens_row = operands
        weights = collect(shards)
        outcome, grads = run_layer(weights, shards, rows, upward, lens_row, features)
        grads = settle(grads)
        totals = tuple((total + member for total, member in zip(totals, grads)))
        return (totals, outcome)

    totals = tuple((jnp.zeros(piece.shape, jnp.float32) for piece in shards))
    totals, outcome = lax.scan(process, totals, (stream, upstream, lengths))
    output = outcome[0].reshape(micro_count * seq_len, D)
    input_grad = outcome[1].reshape(micro_count * seq_len, D)
    return (
        output,
        input_grad,
        totals[0],
        totals[1],
        totals[2],
        totals[3],
        totals[4],
        totals[5],
        totals[6],
        totals[7],
        totals[8],
        totals[9],
        totals[10],
        totals[11],
        totals[12],
        totals[13],
        totals[14],
        totals[15],
    )


def solution(mesh):
    in_specs = (
        P(("wide", "narrow"), None),
        P(("wide", "narrow"), None),
        P(("wide", "narrow"), None),
        P(),
        P("wide"),
        P("wide"),
        P("wide", None),
        P("wide"),
        P("wide", None),
        P("wide"),
        P("wide", None),
        P("wide"),
        P("wide", None),
        P("wide"),
        P("wide"),
        P("wide"),
        P("wide", None),
        P("wide"),
        P("wide", None),
        P("wide"),
    )
    out_specs = (
        P(("wide", "narrow"), None),
        P(("wide", "narrow"), None),
        P("wide"),
        P("wide"),
        P("wide", None),
        P("wide"),
        P("wide", None),
        P("wide"),
        P("wide", None),
        P("wide"),
        P("wide", None),
        P("wide"),
        P("wide"),
        P("wide"),
        P("wide", None),
        P("wide"),
        P("wide", None),
        P("wide"),
    )
    return jax.shard_map(
        on_device, mesh=mesh, in_specs=in_specs, out_specs=out_specs, check_vma=False
    )
```

profile of v0, /device:TPU:0, one launch (start us, length us, event | category | flops | bytes accessed | tf_op | source)
XLA Modules:
  0.0 1814.6 jit_solution(2300165558334829276)
XLA Ops:
  9.0 1798.8 %while.82 = (s32[]{:T(128)}, f32[96]{0:T(128)}, f32[96]{0:T(128)}, f32[96,768]{1,0:T(8,128)}, f32[96]{0:T(128)}, /*index=5*/f32[96,768]{1,0:T(8,128)}, f32[96]{0...) while((s32[]{:T(128)}, f32[96]{0:T(128)}, f32[96]{0:T(128)}, ...), condition=%wide.region_60.61_spmd.clone.clone, body=%wide.region_0.60_spmd.clone.sunk.clone | while | flops 45781344256 | bytes 794361152 | solution.py:343
  24.8 25.7 %all-reduce.44 = (bf16[768]{0:T(1024)(128)(2,1)S(1)}, bf16[768]{0:T(1024)(128)(2,1)S(1)}, bf16[768]{0:T(1024)(128)(2,1)S(1)}, bf16[768]{0:T(1024)(128)(2,1)S(1)}...) all-reduce(bf16[768]{0:T(1024)(128)(2,1)S(1)} %dynamic-update-slice, ...), channel_id=1, replica_groups=mesh['wide'=8,'narrow'=4] {'wide'}, use_global_device_ids=true, to_apply=%add.6 | all-reduce | flops 6912 | bytes 27648 | tf_op jit(solution)/shard_map/while
  54.2 8.1 all-gather.4
  96.3 51.7 %while.80 = (s32[]{:T(128)}, f32[12,1024,64]{1,2,0:T(8,128)}, f32[12,1024]{1,0:T(8,128)S(1)}, bf16[12,1024,32]{2,1,0:T(8,128)(2,1)}, bf16[12,1024,32]{2,1,0:T(8,...) while((s32[]{:T(128)}, f32[12,1024,64]{1,2,0:T(8,128)}, ...), condition=%wide.region_8.8_spmd.clone, body=%wide.region_6.7_spmd.clone.sunk | while | flops 211811328 | bytes 5273697 | solution.py:200
  156.9 38.1 %multiply_convert_fusion.7 = (bf16[1024,3072]{1,0:T(8,128)(2,1)}, f32[1024,3072]{1,0:T(8,128)}, f32[1024,3072]{1,0:T(8,128)}) fusion(f32[3072]{0:T(1024)S(1)} %bitcast.499, bf16[768,3072]{1,0:T(8,128)(2,1)} %all-gather.26.cloned.1.call-done, f32[1024,768]{0,1:T(8,128)} %copy-done.3, f32[768]{0:T(1024)S(1)} %convert_element_type.664, ...), kind=kOutput, calls=%fused_computation.64.clone.1.clone | convolution fusion | flops 5043388416 | bytes 39348224 | tf_op jit(solution)/shard_map/while/body/eval_jaxpr/dot_general | solution.py:213
  197.4 9.6 add_add_fusion.7
  216.7 29.3 %all-gather.34.cloned.1.call-done = bf16[3072,768]{1,0:T(8,128)(2,1)} async-done(((bf16[384,768]{1,0:T(8,128)(2,1)}), bf16[3072,768]{1,0:T(8,128)(2,1)}) %all-gather.34.cloned.1.call-update) | async-done | bytes 4718608 | tf_op jit(solution)/shard_map/while/body/eval_jaxpr/all_gather | solution.py:88
  246.0 18.7 %convert_reduce_fusion.24 = (f32[3072]{0:T(1024)S(1)}, bf16[1024,3072]{1,0:T(8,128)(2,1)}) fusion(f32[1024,3072]{1,0:T(8,128)} %get-tuple-element.1641, bf16[3072,768]{1,0:T(8,128)(2,1)} %all-gather.34.cloned.1.call-done, bf16[1,1024,768]{2,1,0:T(8,128)(2,1)} %constant_dynamic-slice_fusion.14, f32[1024,3072]{1,0:T(8,128)} %get-tuple-element.1643, ...), kind=kOutput, calls=%fused_computation.62.clone.1.clone | convolution fusion | flops 4885312512 | bytes 37773312 | tf_op jit(solution)/shard_map/while/body/eval_jaxpr/dot_general | solution.py:63
  264.7 22.0 %all-gather.36.cloned.1.call-done = bf16[768,3072]{1,0:T(8,128)(2,1)} async-done(((bf16[96,3072]{1,0:T(8,128)(2,1)}), bf16[768,3072]{1,0:T(8,128)(2,1)}) %all-gather.36.cloned.1.call-update) | async-done | bytes 4718608 | tf_op jit(solution)/shard_map/while/body/eval_jaxpr/all_gather | solution.py:86
  286.7 9.7 fusion.418
  306.1 6.4 all-gather.32.cloned.1.call-done
  316.9 5.9 copy.152
  322.8 147.8 %while.81 = (s32[]{:T(128)}, f32[12,1024,32]{1,2,0:T(8,128)}, f32[12,1024,32]{1,2,0:T(8,128)}, bf16[12,1024,64]{1,2,0:T(8,128)(2,1)S(1)}, f32[12,1024,64]{2,1,0:...) while((s32[]{:T(128)}, f32[12,1024,32]{1,2,0:T(8,128)}, ...), condition=%wide.region_15.15_spmd.clone, body=%wide.region_13.14_spmd.clone.sunk | while | flops 481888256 | bytes 10818697 | solution.py:248
  502.1 9.9 fusion.431
  512.1 10.6 fusion.430
  549.5 25.8 %reduce-scatter.7.cloned.1.call-done = f32[96,768]{1,0:T(8,128)} async-done(((f32[768,768]{1,0:T(8,128)}), f32[96,768]{1,0:T(8,128)}) %reduce-scatter.7.cloned.1.call-update) | async-done | bytes 294928 | tf_op jit(solution)/shard_map/while/body/eval_jaxpr/reduce_scatter | solution.py:97
  577.0 43.9 %reduce-scatter.13.cloned.1.call-done = f32[96,768]{1,0:T(8,128)} async-done(((f32[768,768]{1,0:T(8,128)}), f32[96,768]{1,0:T(8,128)}) %reduce-scatter.13.cloned.1.call-update) | async-done | bytes 294928 | tf_op jit(solution)/shard_map/while/body/eval_jaxpr/reduce_scatter | solution.py:103
  622.5 43.9 %reduce-scatter.11.cloned.1.call-done = f32[96,768]{1,0:T(8,128)} async-done(((f32[768,768]{1,0:T(8,128)}), f32[96,768]{1,0:T(8,128)}) %reduce-scatter.11.cloned.1.call-update) | async-done | bytes 294928 | tf_op jit(solution)/shard_map/while/body/eval_jaxpr/reduce_scatter | solution.py:101
  668.1 78.5 %reduce-scatter.17.cloned.1.call-done = f32[384,768]{1,0:T(8,128)} async-done(((f32[3072,768]{1,0:T(8,128)}), f32[384,768]{1,0:T(8,128)}) %reduce-scatter.17.cloned.1.call-update) | async-done | bytes 1179664 | tf_op jit(solution)/shard_map/while/body/eval_jaxpr/reduce_scatter | solution.py:109
  748.8 78.1 %reduce-scatter.15.cloned.1.call-done = f32[96,3072]{1,0:T(8,128)} async-done(((f32[768,3072]{1,0:T(8,128)}), f32[96,3072]{1,0:T(8,128)}) %reduce-scatter.15.cloned.1.call-update) | async-done | bytes 1179664 | tf_op jit(solution)/shard_map/while/body/eval_jaxpr/reduce_scatter | solution.py:107
  829.0 6.0 add_bitcast_fusion.3
  836.9 25.0 %all-reduce.45 = (bf16[768]{0:T(1024)(128)(2,1)S(1)}, bf16[768]{0:T(1024)(128)(2,1)S(1)}, bf16[768]{0:T(1024)(128)(2,1)S(1)}, bf16[768]{0:T(1024)(128)(2,1)S(1)}...) all-reduce(f32[768]{0:T(1024)S(1)} %get-tuple-element.1666, ...), channel_id=2, replica_groups=mesh['wide'=8,'narrow'=4] {'wide'}, use_global_device_ids=true, to_apply=%region_17.17.clone | all-reduce | flops 9984 | bytes 59904 | tf_op jit(solution)/shard_map/while
  865.1 12.0 all-reduce.46
  879.4 26.1 %all-reduce.50.cloned.1.call-done = (bf16[96,768]{1,0:T(8,128)(2,1)}, bf16[96,768]{1,0:T(8,128)(2,1)}, bf16[96,768]{1,0:T(8,128)(2,1)}, bf16[96,768]{1,0:T(8,128...) async-done(((bf16[96,768]{1,0:T(8,128)(2,1)}, bf16[96,768]{1,0:T(8,128)(2,1)}, bf16[96,768]{1,0:T(8,128)(2,1)}, bf16[96,768]{1,0:T(8,128)(2,1)}, ...) | async-done | bytes 1769488 | tf_op jit(solution)/shard_map/while/body/eval_jaxpr/psum | solution.py:115
  925.4 23.8 %all-reduce.44 = (bf16[768]{0:T(1024)(128)(2,1)S(1)}, bf16[768]{0:T(1024)(128)(2,1)S(1)}, bf16[768]{0:T(1024)(128)(2,1)S(1)}, bf16[768]{0:T(1024)(128)(2,1)S(1)}...) all-reduce(bf16[768]{0:T(1024)(128)(2,1)S(1)} %dynamic-update-slice, ...), channel_id=1, replica_groups=mesh['wide'=8,'narrow'=4] {'wide'}, use_global_device_ids=true, to_apply=%add.6 | all-reduce | flops 6912 | bytes 27648 | tf_op jit(solution)/shard_map/while
  952.9 8.0 all-gather.4
  994.2 51.8 %while.80 = (s32[]{:T(128)}, f32[12,1024,64]{1,2,0:T(8,128)}, f32[12,1024]{1,0:T(8,128)S(1)}, bf16[12,1024,32]{2,1,0:T(8,128)(2,1)}, bf16[12,1024,32]{2,1,0:T(8,...) while((s32[]{:T(128)}, f32[12,1024,64]{1,2,0:T(8,128)}, ...), condition=%wide.region_8.8_spmd.clone, body=%wide.region_6.7_spmd.clone.sunk | while | flops 211811328 | bytes 5273697 | solution.py:200
  1054.0 38.4 %multiply_convert_fusion.7 = (bf16[1024,3072]{1,0:T(8,128)(2,1)}, f32[1024,3072]{1,0:T(8,128)}, f32[1024,3072]{1,0:T(8,128)}) fusion(f32[3072]{0:T(1024)S(1)} %bitcast.499, bf16[768,3072]{1,0:T(8,128)(2,1)} %all-gather.26.cloned.1.call-done, f32[1024,768]{0,1:T(8,128)} %copy-done.3, f32[768]{0:T(1024)S(1)} %convert_element_type.664, ...), kind=kOutput, calls=%fused_computation.64.clone.1.clone | convolution fusion | flops 5043388416 | bytes 39348224 | tf_op jit(solution)/shard_map/while/body/eval_jaxpr/dot_general | solution.py:213
  1093.9 9.6 add_add_fusion.7
  1113.0 29.5 %all-gather.34.cloned.1.call-done = bf16[3072,768]{1,0:T(8,128)(2,1)} async-done(((bf16[384,768]{1,0:T(8,128)(2,1)}), bf16[3072,768]{1,0:T(8,128)(2,1)}) %all-gather.34.cloned.1.call-update) | async-done | bytes 4718608 | tf_op jit(solution)/shard_map/while/body/eval_jaxpr/all_gather | solution.py:88
  1142.5 18.5 %convert_reduce_fusion.24 = (f32[3072]{0:T(1024)S(1)}, bf16[1024,3072]{1,0:T(8,128)(2,1)}) fusion(f32[1024,3072]{1,0:T(8,128)} %get-tuple-element.1641, bf16[3072,768]{1,0:T(8,128)(2,1)} %all-gather.34.cloned.1.call-done, bf16[1,1024,768]{2,1,0:T(8,128)(2,1)} %constant_dynamic-slice_fusion.14, f32[1024,3072]{1,0:T(8,128)} %get-tuple-element.1643, ...), kind=kOutput, calls=%fused_computation.62.clone.1.clone | convolution fusion | flops 4885312512 | bytes 37773312 | tf_op jit(solution)/shard_map/while/body/eval_jaxpr/dot_general | solution.py:63
  1161.0 22.0 %all-gather.36.cloned.1.call-done = bf16[768,3072]{1,0:T(8,128)(2,1)} async-done(((bf16[96,3072]{1,0:T(8,128)(2,1)}), bf16[768,3072]{1,0:T(8,128)(2,1)}) %all-gather.36.cloned.1.call-update) | async-done | bytes 4718608 | tf_op jit(solution)/shard_map/while/body/eval_jaxpr/all_gather | solution.py:86
  1183.0 9.7 fusion.418
  1202.4 6.4 all-gather.32.cloned.1.call-done
  1213.2 5.9 copy.152
  1219.1 147.8 %while.81 = (s32[]{:T(128)}, f32[12,1024,32]{1,2,0:T(8,128)}, f32[12,1024,32]{1,2,0:T(8,128)}, bf16[12,1024,64]{1,2,0:T(8,128)(2,1)S(1)}, f32[12,1024,64]{2,1,0:...) while((s32[]{:T(128)}, f32[12,1024,32]{1,2,0:T(8,128)}, ...), condition=%wide.region_15.15_spmd.clone, body=%wide.region_13.14_spmd.clone.sunk | while | flops 481888256 | bytes 10818697 | solution.py:248
  1367.0 5.7 convolution_bitcast_fusion.9
  1398.6 9.9 fusion.431
  1408.6 10.6 fusion.430
  1445.8 25.9 %reduce-scatter.7.cloned.1.call-done = f32[96,768]{1,0:T(8,128)} async-done(((f32[768,768]{1,0:T(8,128)}), f32[96,768]{1,0:T(8,128)}) %reduce-scatter.7.cloned.1.call-update) | async-done | bytes 294928 | tf_op jit(solution)/shard_map/while/body/eval_jaxpr/reduce_scatter | solution.py:97
  1473.4 44.1 %reduce-scatter.13.cloned.1.call-done = f32[96,768]{1,0:T(8,128)} async-done(((f32[768,768]{1,0:T(8,128)}), f32[96,768]{1,0:T(8,128)}) %reduce-scatter.13.cloned.1.call-update) | async-done | bytes 294928 | tf_op jit(solution)/shard_map/while/body/eval_jaxpr/reduce_scatter | solution.py:103
  1519.1 44.1 %reduce-scatter.11.cloned.1.call-done = f32[96,768]{1,0:T(8,128)} async-done(((f32[768,768]{1,0:T(8,128)}), f32[96,768]{1,0:T(8,128)}) %reduce-scatter.11.cloned.1.call-update) | async-done | bytes 294928 | tf_op jit(solution)/shard_map/while/body/eval_jaxpr/reduce_scatter | solution.py:101
  1564.8 78.6 %reduce-scatter.17.cloned.1.call-done = f32[384,768]{1,0:T(8,128)} async-done(((f32[3072,768]{1,0:T(8,128)}), f32[384,768]{1,0:T(8,128)}) %reduce-scatter.17.cloned.1.call-update) | async-done | bytes 1179664 | tf_op jit(solution)/shard_map/while/body/eval_jaxpr/reduce_scatter | solution.py:109
  1645.5 78.1 %reduce-scatter.15.cloned.1.call-done = f32[96,3072]{1,0:T(8,128)} async-done(((f32[768,3072]{1,0:T(8,128)}), f32[96,3072]{1,0:T(8,128)}) %reduce-scatter.15.cloned.1.call-update) | async-done | bytes 1179664 | tf_op jit(solution)/shard_map/while/body/eval_jaxpr/reduce_scatter | solution.py:107
  1725.7 6.0 add_bitcast_fusion.3
  1733.6 25.0 %all-reduce.45 = (bf16[768]{0:T(1024)(128)(2,1)S(1)}, bf16[768]{0:T(1024)(128)(2,1)S(1)}, bf16[768]{0:T(1024)(128)(2,1)S(1)}, bf16[768]{0:T(1024)(128)(2,1)S(1)}...) all-reduce(f32[768]{0:T(1024)S(1)} %get-tuple-element.1666, ...), channel_id=2, replica_groups=mesh['wide'=8,'narrow'=4] {'wide'}, use_global_device_ids=true, to_apply=%region_17.17.clone | all-reduce | flops 9984 | bytes 59904 | tf_op jit(solution)/shard_map/while
  1761.7 12.0 all-reduce.46
  1776.1 26.1 %all-reduce.50.cloned.1.call-done = (bf16[96,768]{1,0:T(8,128)(2,1)}, bf16[96,768]{1,0:T(8,128)(2,1)}, bf16[96,768]{1,0:T(8,128)(2,1)}, bf16[96,768]{1,0:T(8,128...) async-done(((bf16[96,768]{1,0:T(8,128)(2,1)}, bf16[96,768]{1,0:T(8,128)(2,1)}, bf16[96,768]{1,0:T(8,128)(2,1)}, bf16[96,768]{1,0:T(8,128)(2,1)}, ...) | async-done | bytes 1769488 | tf_op jit(solution)/shard_map/while/body/eval_jaxpr/psum | solution.py:115
  (954 shorter events, 718.9 us)
Async XLA Ops:
  9.5 53.4 %all-gather.20.cloned.1.call-start = ((), (), s32[]{:S(2)}) async-start(), calls=%async_computation.7 | async-start | bytes 1327104 | tf_op jit(solution)/shard_map/while/body/eval_jaxpr/all_gather | solution.py:76
  10.2 57.3 %all-gather.18.cloned.1.call-start = ((), (), s32[]{:S(2)}) async-start(), calls=%async_computation.6 | async-start | bytes 1327104 | tf_op jit(solution)/shard_map/while/body/eval_jaxpr/all_gather | solution.py:78
  11.0 79.7 %all-gather.22.cloned.1.call-start = ((), (), s32[]{:S(2)}) async-start(), calls=%async_computation.8 | async-start | bytes 1327104 | tf_op jit(solution)/shard_map/while/body/eval_jaxpr/all_gather | solution.py:80
  11.7 138.8 %all-gather.24.cloned.1.call-start = ((), (), s32[]{:S(2)}) async-start(), calls=%async_computation.9 | async-start | bytes 1327104 | tf_op jit(solution)/shard_map/while/body/eval_jaxpr/all_gather | solution.py:82
  12.3 144.6 %all-gather.26.cloned.1.call-start = ((), (), s32[]{:S(2)}) async-start(), calls=%async_computation.10 | async-start | bytes 5308416 | tf_op jit(solution)/shard_map/while/body/eval_jaxpr/all_gather | solution.py:86
  12.9 184.6 %all-gather.28.cloned.1.call-start = ((), (), s32[]{:S(2)}) async-start(), calls=%async_computation.11 | async-start | bytes 5308416 | tf_op jit(solution)/shard_map/while/body/eval_jaxpr/all_gather | solution.py:88
  13.4 232.5 %all-gather.34.cloned.1.call-start = ((), (), s32[]{:S(2)}) async-start(), calls=%async_computation.14 | async-start | bytes 5308416 | tf_op jit(solution)/shard_map/while/body/eval_jaxpr/all_gather | solution.py:88
  52.9 97.6 %copy-start = (bf16[1,1024,768]{1,2,0:T(8,128)(2,1)}, bf16[1,1024,768]{1,2,0:T(8,128)(2,1)S(1)}, u32[]{:S(2)}) copy-start(bf16[1,1024,768]{1,2,0:T(8,128)(2,1)S(1)} %copy.145) | copy-start | bytes 4718596 | tf_op jit(solution)/shard_map/while
  53.7 94.4 %copy-start.36 = (f32[1024]{0:T(1024)}, f32[1024]{0:T(1024)S(1)}, u32[]{:S(2)}) copy-start(f32[1024]{0:T(1024)S(1)} %compare_convert_fusion.3) | copy-start | bytes 12292 | tf_op jit(solution)/shard_map/while
  207.0 79.6 %all-gather.36.cloned.1.call-start = ((), (), s32[]{:S(2)}) async-start(), calls=%async_computation.15 | async-start | bytes 5308416 | tf_op jit(solution)/shard_map/while/body/eval_jaxpr/all_gather | solution.py:86
  207.8 104.7 %all-gather.32.cloned.1.call-start = ((), (), s32[]{:S(2)}) async-start(), calls=%async_computation.13 | async-start | bytes 1327104 | tf_op jit(solution)/shard_map/while/body/eval_jaxpr/all_gather | solution.py:82
  208.5 321.2 %all-gather.40.cloned.1.call-start = ((), (), s32[]{:S(2)}) async-start(), calls=%async_computation.17 | async-start | bytes 1327104 | tf_op jit(solution)/shard_map/while/body/eval_jaxpr/all_gather | solution.py:78
  209.1 325.5 %all-gather.38.cloned.1.call-start = ((), (), s32[]{:S(2)}) async-start(), calls=%async_computation.16 | async-start | bytes 1327104 | tf_op jit(solution)/shard_map/while/body/eval_jaxpr/all_gather | solution.py:76
  209.8 329.5 %all-gather.30.cloned.1.call-start = ((), (), s32[]{:S(2)}) async-start(), calls=%async_computation.12 | async-start | bytes 1327104 | tf_op jit(solution)/shard_map/while/body/eval_jaxpr/all_gather | solution.py:80
  216.6 331.3 %reduce-scatter.9.cloned.1.call-start = ((), (), s32[]{:S(2)}) async-start(), calls=%async_computation.19 | async-start | bytes 2654208 | tf_op jit(solution)/shard_map/while/body/eval_jaxpr/reduce_scatter | solution.py:99
  322.8 147.9 %copy-start.26 = (f32[64,384]{0,1:T(8,128)S(1)}, f32[64,384]{0,1:T(8,128)}, u32[]{:S(2)}) copy-start(f32[64,384]{0,1:T(8,128)} %get-tuple-element.1969) | copy-start | bytes 294916 | tf_op jit(solution)/shard_map/while
  470.6 68.7 %copy-start.10 = (bf16[12,1024,64]{1,2,0:T(8,128)(2,1)}, bf16[12,1024,64]{1,2,0:T(8,128)(2,1)S(1)}, u32[]{:S(2)}) copy-start(bf16[12,1024,64]{1,2,0:T(8,128)(2,1)S(1)} %get-tuple-element.1653) | copy-start | bytes 4718596 | tf_op jit(solution)/shard_map/while
  487.4 87.9 %reduce-scatter.7.cloned.1.call-start = ((), (), s32[]{:S(2)}) async-start(), calls=%async_computation.18 | async-start | bytes 2654208 | tf_op jit(solution)/shard_map/while/body/eval_jaxpr/reduce_scatter | solution.py:97
  494.0 126.9 %reduce-scatter.13.cloned.1.call-start = ((), (), s32[]{:S(2)}) async-start(), calls=%async_computation.21 | async-start | bytes 2654208 | tf_op jit(solution)/shard_map/while/body/eval_jaxpr/reduce_scatter | solution.py:103
  499.0 167.5 %reduce-scatter.11.cloned.1.call-start = ((), (), s32[]{:S(2)}) async-start(), calls=%async_computation.20 | async-start | bytes 2654208 | tf_op jit(solution)/shard_map/while/body/eval_jaxpr/reduce_scatter | solution.py:101
  502.1 244.6 %reduce-scatter.17.cloned.1.call-start = ((), (), s32[]{:S(2)}) async-start(), calls=%async_computation.23 | async-start | bytes 10616832 | tf_op jit(solution)/shard_map/while/body/eval_jaxpr/reduce_scatter | solution.py:109
  512.1 314.8 %reduce-scatter.15.cloned.1.call-start = ((), (), s32[]{:S(2)}) async-start(), calls=%async_computation.22 | async-start | bytes 10616832 | tf_op jit(solution)/shard_map/while/body/eval_jaxpr/reduce_scatter | solution.py:107
  522.7 382.8 %all-reduce.50.cloned.1.call-start = ((), (), s32[]{:S(2)}) async-start(), calls=%async_computation.24 | async-start | bytes 3538944 | tf_op jit(solution)/shard_map/while/body/eval_jaxpr/psum | solution.py:115
  577.0 252.0 %copy-start.8 = (bf16[1,1024,768]{1,2,0:T(8,128)(2,1)S(1)}, bf16[1,1024,768]{1,2,0:T(8,128)(2,1)}, u32[]{:S(2)}) copy-start(bf16[1,1024,768]{1,2,0:T(8,128)(2,1)} %copy.151) | copy-start | bytes 4718596 | tf_op jit(solution)/shard_map/while
  909.9 51.6 %all-gather.20.cloned.1.call-start = ((), (), s32[]{:S(2)}) async-start(), calls=%async_computation.7 | async-start | bytes 1327104 | tf_op jit(solution)/shard_map/while/body/eval_jaxpr/all_gather | solution.py:76
  910.4 55.6 %all-gather.18.cloned.1.call-start = ((), (), s32[]{:S(2)}) async-start(), calls=%async_computation.6 | async-start | bytes 1327104 | tf_op jit(solution)/shard_map/while/body/eval_jaxpr/all_gather | solution.py:78
  911.2 77.3 %all-gather.22.cloned.1.call-start = ((), (), s32[]{:S(2)}) async-start(), calls=%async_computation.8 | async-start | bytes 1327104 | tf_op jit(solution)/shard_map/while/body/eval_jaxpr/all_gather | solution.py:80
  911.9 136.5 %all-gather.24.cloned.1.call-start = ((), (), s32[]{:S(2)}) async-start(), calls=%async_computation.9 | async-start | bytes 1327104 | tf_op jit(solution)/shard_map/while/body/eval_jaxpr/all_gather | solution.py:82
  912.7 141.3 %all-gather.26.cloned.1.call-start = ((), (), s32[]{:S(2)}) async-start(), calls=%async_computation.10 | async-start | bytes 5308416 | tf_op jit(solution)/shard_map/while/body/eval_jaxpr/all_gather | solution.py:86
  913.2 180.7 %all-gather.28.cloned.1.call-start = ((), (), s32[]{:S(2)}) async-start(), calls=%async_computation.11 | async-start | bytes 5308416 | tf_op jit(solution)/shard_map/while/body/eval_jaxpr/all_gather | solution.py:88
  914.0 228.5 %all-gather.34.cloned.1.call-start = ((), (), s32[]{:S(2)}) async-start(), calls=%async_computation.14 | async-start | bytes 5308416 | tf_op jit(solution)/shard_map/while/body/eval_jaxpr/all_gather | solution.py:88
  951.5 96.9 %copy-start = (bf16[1,1024,768]{1,2,0:T(8,128)(2,1)}, bf16[1,1024,768]{1,2,0:T(8,128)(2,1)S(1)}, u32[]{:S(2)}) copy-start(bf16[1,1024,768]{1,2,0:T(8,128)(2,1)S(1)} %copy.145) | copy-start | bytes 4718596 | tf_op jit(solution)/shard_map/while
  952.3 93.7 %copy-start.36 = (f32[1024]{0:T(1024)}, f32[1024]{0:T(1024)S(1)}, u32[]{:S(2)}) copy-start(f32[1024]{0:T(1024)S(1)} %compare_convert_fusion.3) | copy-start | bytes 12292 | tf_op jit(solution)/shard_map/while
  1103.5 79.5 %all-gather.36.cloned.1.call-start = ((), (), s32[]{:S(2)}) async-start(), calls=%async_computation.15 | async-start | bytes 5308416 | tf_op jit(solution)/shard_map/while/body/eval_jaxpr/all_gather | solution.py:86
  1104.1 104.7 %all-gather.32.cloned.1.call-start = ((), (), s32[]{:S(2)}) async-start(), calls=%async_computation.13 | async-start | bytes 1327104 | tf_op jit(solution)/shard_map/while/body/eval_jaxpr/all_gather | solution.py:82
  1104.9 321.1 %all-gather.40.cloned.1.call-start = ((), (), s32[]{:S(2)}) async-start(), calls=%async_computation.17 | async-start | bytes 1327104 | tf_op jit(solution)/shard_map/while/body/eval_jaxpr/all_gather | solution.py:78
  1105.6 325.2 %all-gather.38.cloned.1.call-start = ((), (), s32[]{:S(2)}) async-start(), calls=%async_computation.16 | async-start | bytes 1327104 | tf_op jit(solution)/shard_map/while/body/eval_jaxpr/all_gather | solution.py:76
  1106.2 329.5 %all-gather.30.cloned.1.call-start = ((), (), s32[]{:S(2)}) async-start(), calls=%async_computation.12 | async-start | bytes 1327104 | tf_op jit(solution)/shard_map/while/body/eval_jaxpr/all_gather | solution.py:80
  1112.9 331.2 %reduce-scatter.9.cloned.1.call-start = ((), (), s32[]{:S(2)}) async-start(), calls=%async_computation.19 | async-start | bytes 2654208 | tf_op jit(solution)/shard_map/while/body/eval_jaxpr/reduce_scatter | solution.py:99
  1219.1 147.8 %copy-start.26 = (f32[64,384]{0,1:T(8,128)S(1)}, f32[64,384]{0,1:T(8,128)}, u32[]{:S(2)}) copy-start(f32[64,384]{0,1:T(8,128)} %get-tuple-element.1969) | copy-start | bytes 294916 | tf_op jit(solution)/shard_map/while
  1366.9 68.7 %copy-start.10 = (bf16[12,1024,64]{1,2,0:T(8,128)(2,1)}, bf16[12,1024,64]{1,2,0:T(8,128)(2,1)S(1)}, u32[]{:S(2)}) copy-start(bf16[12,1024,64]{1,2,0:T(8,128)(2,1)S(1)} %get-tuple-element.1653) | copy-start | bytes 4718596 | tf_op jit(solution)/shard_map/while
  1383.7 88.0 %reduce-scatter.7.cloned.1.call-start = ((), (), s32[]{:S(2)}) async-start(), calls=%async_computation.18 | async-start | bytes 2654208 | tf_op jit(solution)/shard_map/while/body/eval_jaxpr/reduce_scatter | solution.py:97
  1390.4 127.0 %reduce-scatter.13.cloned.1.call-start = ((), (), s32[]{:S(2)}) async-start(), calls=%async_computation.21 | async-start | bytes 2654208 | tf_op jit(solution)/shard_map/while/body/eval_jaxpr/reduce_scatter | solution.py:103
  1395.5 167.7 %reduce-scatter.11.cloned.1.call-start = ((), (), s32[]{:S(2)}) async-start(), calls=%async_computation.20 | async-start | bytes 2654208 | tf_op jit(solution)/shard_map/while/body/eval_jaxpr/reduce_scatter | solution.py:101
  1398.6 244.7 %reduce-scatter.17.cloned.1.call-start = ((), (), s32[]{:S(2)}) async-start(), calls=%async_computation.23 | async-start | bytes 10616832 | tf_op jit(solution)/shard_map/while/body/eval_jaxpr/reduce_scatter | solution.py:109
  1408.6 315.0 %reduce-scatter.15.cloned.1.call-start = ((), (), s32[]{:S(2)}) async-start(), calls=%async_computation.22 | async-start | bytes 10616832 | tf_op jit(solution)/shard_map/while/body/eval_jaxpr/reduce_scatter | solution.py:107
  1419.2 383.0 %all-reduce.50.cloned.1.call-start = ((), (), s32[]{:S(2)}) async-start(), calls=%async_computation.24 | async-start | bytes 3538944 | tf_op jit(solution)/shard_map/while/body/eval_jaxpr/psum | solution.py:115
  1473.3 252.4 %copy-start.8 = (bf16[1,1024,768]{1,2,0:T(8,128)(2,1)S(1)}, bf16[1,1024,768]{1,2,0:T(8,128)(2,1)}, u32[]{:S(2)}) copy-start(bf16[1,1024,768]{1,2,0:T(8,128)(2,1)} %copy.151) | copy-start | bytes 4718596 | tf_op jit(solution)/shard_map/while
  (142 other events, 1478.6 us)
Sparse Core Ops, SparseCore 0:
  12.2 26.7 all-gather.19
  40.8 23.9 all-gather.17
  66.7 23.9 all-gather.21
  92.4 23.9 all-gather.23
  118.1 38.7 all-gather.25
  158.6 38.7 all-gather.27
  207.1 38.7 all-gather.33
  247.8 38.7 all-gather.35
  288.6 23.9 all-gather.31
  314.2 23.9 all-gather.39
  340.1 23.9 all-gather.37
  365.8 23.9 all-gather.29
  487.5 42.1 reduce-scatter.8
  532.9 42.3 reduce-scatter.6
  578.5 42.3 reduce-scatter.12
  624.1 42.3 reduce-scatter.10
  669.8 76.7 reduce-scatter.16
  750.0 76.8 reduce-scatter.14
  829.7 75.7 all-reduce.49
  912.2 22.7 all-gather.19
  937.0 23.9 all-gather.17
  962.9 23.8 all-gather.21
  988.7 23.9 all-gather.23
  1014.4 38.7 all-gather.25
  1055.1 38.7 all-gather.27
  1103.6 38.7 all-gather.33
  1144.2 38.7 all-gather.35
  1184.9 23.9 all-gather.31
  1210.7 23.9 all-gather.39
  1236.4 23.9 all-gather.37
  1262.3 23.9 all-gather.29
  1383.8 42.2 reduce-scatter.8
  1429.3 42.3 reduce-scatter.6
  1475.1 42.3 reduce-scatter.12
  1520.8 42.3 reduce-scatter.10
  1566.5 76.8 reduce-scatter.16
  1646.7 76.8 reduce-scatter.14
  1726.4 75.7 all-reduce.49
where the time goes:
time: 1830 us; the launch traced here: 1810 us
  waiting for transfers between devices  728 us (40%)
  matrix products  639 us (35%)
  local copies, waits for them, and re-layouts  164 us (9%)
  blocking collectives  140 us (8%)
  other arithmetic  117 us (6%)
    dot_general x60, matrix products, times_transposed(): lax.dot_general(left, right, (((1,), (1,)), ((), ())), preferred_element_...  191 us
    dot_general x60, matrix products, contract_rows(): lax.dot_general(left, right, (((0,), (0,)), ((), ())), preferred_element_...  177 us
    reduce_scatter x2, waiting for transfers between devices, settle(): lax.psum_scatter(grads[14], 'wide', scatter_dimension=0, tiled=True)  157 us
    reduce_scatter x2, waiting for transfers between devices, settle(): lax.psum_scatter(grads[12], 'wide', scatter_dimension=0, tiled=True)  156 us
    while x4, blocking collectives  99.4 us
    reduce_scatter x2, waiting for transfers between devices, settle(): lax.psum_scatter(grads[6], 'wide', scatter_dimension=0, tiled=True)  88 us
    reduce_scatter x2, waiting for transfers between devices, settle(): lax.psum_scatter(grads[8], 'wide', scatter_dimension=0, tiled=True)  88 us
    dot_general x2, matrix products, run_layer(): jnp.dot(hidden_two, up_mat, preferred_element_type=jnp.float32)  76.5 us
  transfers between devices with their start and end apart: 38, of which 22 were waited for; matrix products, arithmetic and copies ran while one was open for 48% of the time, Pallas kernels for 0%

commit v1 on v0

--- a/solution.py
+++ b/solution.py
@@ -12,6 +12,19 @@
 SEGS = 24
 EPSILON = 1e-05
 HIGHEST = lax.Precision.HIGHEST
+
+
+def gather_around(x, axis, dim):
+    ways = lax.axis_size(axis)
+    up = [(d, (d + 1) % ways) for d in range(ways)]
+    down = [(d, (d - 1) % ways) for d in range(ways)]
+    earlier, later = ([x], [x])
+    for _ in range(ways // 2):
+        earlier.append(lax.ppermute(earlier[-1], axis, up))
+    for _ in range((ways - 1) // 2):
+        later.append(lax.ppermute(later[-1], axis, down))
+    line = jnp.concatenate([*earlier[::-1], *later[1:]], axis=dim)
+    return jnp.roll(line, (lax.axis_index(axis) - ways // 2) * x.shape[dim], axis=dim)
 
 
 def pieces(lens_row, seq_len):
@@ -83,7 +96,7 @@
         lax.all_gather(shards[9], "wide", axis=0, tiled=True),
         lax.all_gather(shards[10], "wide", axis=0, tiled=True),
         lax.all_gather(shards[11], "wide", axis=0, tiled=True),
-        lax.all_gather(shards[12], "wide", axis=0, tiled=True),
+        gather_around(shards[12], "wide", 0),
         lax.all_gather(shards[13], "wide", axis=0, tiled=True),
         lax.all_gather(shards[14], "wide", axis=0, tiled=True),
         lax.all_gather(shards[15], "wide", axis=0, tiled=True),

time: 1830 us -> 1790 us (0.978)
  waiting for transfers between devices: 728 us -> 649 us
  starting transfers between devices: 2.7 us -> 26 us
    ppermute x0 -> x21, waiting for transfers between devices: none -> 173 us  [the longest x12 173 us: gather_around(): earlier.append(lax.ppermute(earlier[-1], axis, up))]
    reduce_scatter x2, waiting for transfers between devices: 157 us -> 0.01 us  [settle(): lax.psum_scatter(grads[14], 'wide', scatter_dimension=0, tiled=True)]
    all_gather x4, waiting for transfers between devices: 62.8 us -> 0.01 us  [collect(): lax.all_gather(shards[14], 'wide', axis=0, tiled=True)]
    all_gather x4 -> x0, waiting for transfers between devices: 44.9 us -> none  [collect(): lax.all_gather(shards[12], 'wide', axis=0, tiled=True)]
    ppermute x0 -> x21, starting transfers between devices: none -> 23.4 us  [the longest x9 22.2 us: gather_around(): later.append(lax.ppermute(later[-1], axis, down))]
    while x368 -> x458, local copies, waits for them, and re-layouts: 53.2 us -> 63.9 us
  transfers between devices with their start and end apart: 38 -> 55, of which waited for: 22 -> 26; matrix products, arithmetic and copies ran while one was open for 48% -> 50% of each run, Pallas kernels for 0% -> 0%
where the time goes in v1:
time: 1790 us; the launch traced here: 1780 us
  waiting for transfers between devices  649 us (36%)
  matrix products  647 us (36%)
  local copies, waits for them, and re-layouts  174 us (10%)
  blocking collectives  140 us (8%)
  other arithmetic  117 us (7%)
  starting transfers between devices  26 us (1%)
    dot_general x60, matrix products, times_transposed(): lax.dot_general(left, right, (((1,), (1,)), ((), ())), preferred_element_...  198 us
    dot_general x60, matrix products, contract_rows(): lax.dot_general(left, right, (((0,), (0,)), ((), ())), preferred_element_...  177 us
    ppermute x12, waiting for transfers between devices, gather_around(): earlier.append(lax.ppermute(earlier[-1], axis, up))  173 us
    reduce_scatter x2, waiting for transfers between devices, settle(): lax.psum_scatter(grads[12], 'wide', scatter_dimension=0, tiled=True)  157 us
    while x4, blocking collectives  96.5 us
    reduce_scatter x2, waiting for transfers between devices, settle(): lax.psum_scatter(grads[8], 'wide', scatter_dimension=0, tiled=True)  88 us
    reduce_scatter x2, waiting for transfers between devices, settle(): lax.psum_scatter(grads[6], 'wide', scatter_dimension=0, tiled=True)  88 us
    dot_general x2, matrix products, run_layer(): jnp.dot(hidden_two, up_mat, preferred_element_type=jnp.float32)  75.9 us
  transfers between devices with their start and end apart: 55, of which 26 were waited for; matrix products, arithmetic and copies ran while one was open for 50% of the time, Pallas kernels for 0%

profile of v1, /device:TPU:0, one launch (start us, length us, event | category | flops | bytes accessed | tf_op | source)
XLA Modules:
  0.0 1778.2 jit_solution(12531102612472812321)
XLA Ops:
  7.7 10.7 collective-permute-done.7
  21.0 12.0 collective-permute-done.8
  35.7 12.6 collective-permute-done.9
  52.7 11.5 collective-permute-done.10
  68.1 1703.0 %while.111 = (s32[]{:T(128)}, f32[96]{0:T(128)}, f32[96]{0:T(128)}, f32[96,768]{1,0:T(8,128)}, f32[96]{0:T(128)}, /*index=5*/f32[96,768]{1,0:T(8,128)}, f32[96]{...) while((s32[]{:T(128)}, f32[96]{0:T(128)}, f32[96]{0:T(128)}, ...), condition=%wide.region_60.62_spmd.clone.clone, body=%wide.region_0.61_spmd.clone.sunk.clone | while | flops 45800218624 | bytes 807403264 | solution.py:356
  75.4 22.8 %all-reduce.44 = (bf16[768]{0:T(1024)(128)(2,1)S(1)}, bf16[768]{0:T(1024)(128)(2,1)S(1)}, bf16[768]{0:T(1024)(128)(2,1)S(1)}, bf16[768]{0:T(1024)(128)(2,1)S(1)}...) all-reduce(bf16[768]{0:T(1024)(128)(2,1)S(1)} %dynamic-update-slice, ...), channel_id=1, replica_groups=mesh['wide'=8,'narrow'=4] {'wide'}, use_global_device_ids=true, to_apply=%add.6 | all-reduce | flops 6912 | bytes 27648 | tf_op jit(solution)/shard_map/while
  101.8 11.7 all-gather.4
  155.7 51.7 %while.109 = (s32[]{:T(128)}, f32[12,1024,64]{1,2,0:T(8,128)}, f32[12,1024]{1,0:T(8,128)S(1)}, bf16[12,1024,32]{2,1,0:T(8,128)(2,1)}, bf16[12,1024,32]{2,1,0:T(8...) while((s32[]{:T(128)}, f32[12,1024,64]{1,2,0:T(8,128)}, ...), condition=%wide.region_8.8_spmd.clone, body=%wide.region_6.7_spmd.clone.sunk | while | flops 211811328 | bytes 5273697 | solution.py:213
  215.1 38.2 %multiply_convert_fusion.7 = (bf16[1024,3072]{1,0:T(8,128)(2,1)}, f32[1024,3072]{1,0:T(8,128)}, f32[1024,3072]{1,0:T(8,128)}) fusion(f32[3072]{0:T(1024)S(1)} %bitcast.491, s32[]{:T(128)S(6)} %select_n.289, bf16[768,3072]{1,0:T(8,128)(2,1)S(1)} %bitcast.494, f32[1024,768]{0,1:T(8,128)S(1)} %get-tuple-element.1939, ...), kind=kOutput, calls=%fused_computation.64.clone.1.clone | convolution fusion | flops 5052825600 | bytes 39348228 | tf_op jit(solution)/shard_map/while/body/eval_jaxpr/dot_general | solution.py:226
  253.3 10.2 add_add_fusion.7
  265.8 10.2 fusion.432
  277.4 10.2 collective-permute-done
  290.3 24.2 %collective-permute-done.1 = bf16[96,3072]{1,0:T(8,128)(2,1)S(1)} collective-permute-done((bf16[96,3072]{1,0:T(8,128)(2,1)S(1)}, bf16[96,3072]{1,0:T(8,128)(2,1)S(1)}, u32[]{:S(2)}, u32[]{:S(2)}) %collective-permute-start.1) | collective-permute-done | bytes 589856 | tf_op jit(solution)/shard_map/while/body/eval_jaxpr/ppermute | solution.py:23
  317.1 14.9 collective-permute-done.2
  337.9 13.7 collective-permute-done.3
  363.2 18.4 %convert_reduce_fusion.24 = (f32[3072]{0:T(1024)S(1)}, bf16[1024,3072]{1,0:T(8,128)(2,1)}) fusion(f32[1024,3072]{1,0:T(8,128)} %get-tuple-element.1947, bf16[3072,768]{1,0:T(8,128)(2,1)} %all-gather.30.cloned.1.call-done, bf16[1,1024,768]{2,1,0:T(8,128)(2,1)S(1)} %constant_dynamic-slice_fusion.14, f32[1024,3072]{1,0:T(8,128)} %get-tuple-element.1949, ...), kind=kOutput, calls=%fused_computation.62.clone.1.clone | convolution fusion | flops 4885312512 | bytes 37773312 | tf_op jit(solution)/shard_map/while/body/eval_jaxpr/dot_general | solution.py:76
  381.7 12.9 fusion.419
  415.2 147.7 %while.110 = (s32[]{:T(128)}, f32[12,1024,32]{1,2,0:T(8,128)}, f32[12,1024,32]{1,2,0:T(8,128)}, bf16[12,1024,64]{1,2,0:T(8,128)(2,1)S(1)}, f32[12,1024,64]{2,1,0...) while((s32[]{:T(128)}, f32[12,1024,32]{1,2,0:T(8,128)}, ...), condition=%wide.region_15.16_spmd.clone, body=%wide.region_13.15_spmd.clone.sunk | while | flops 481888256 | bytes 10818697 | solution.py:261
  595.0 10.6 fusion.431
  634.2 32.9 %reduce-scatter.7.cloned.1.call-done = f32[96,768]{1,0:T(8,128)} async-done(((f32[768,768]{1,0:T(8,128)}), f32[96,768]{1,0:T(8,128)}) %reduce-scatter.7.cloned.1.call-update) | async-done | bytes 294928 | tf_op jit(solution)/shard_map/while/body/eval_jaxpr/reduce_scatter | solution.py:110
  668.7 43.9 %reduce-scatter.13.cloned.1.call-done = f32[96,768]{1,0:T(8,128)} async-done(((f32[768,768]{1,0:T(8,128)}), f32[96,768]{1,0:T(8,128)}) %reduce-scatter.13.cloned.1.call-update) | async-done | bytes 294928 | tf_op jit(solution)/shard_map/while/body/eval_jaxpr/reduce_scatter | solution.py:116
  714.3 43.9 %reduce-scatter.11.cloned.1.call-done = f32[96,768]{1,0:T(8,128)} async-done(((f32[768,768]{1,0:T(8,128)}), f32[96,768]{1,0:T(8,128)}) %reduce-scatter.11.cloned.1.call-update) | async-done | bytes 294928 | tf_op jit(solution)/shard_map/while/body/eval_jaxpr/reduce_scatter | solution.py:114
  759.9 78.5 %reduce-scatter.15.cloned.1.call-done = f32[96,3072]{1,0:T(8,128)} async-done(((f32[768,3072]{1,0:T(8,128)}), f32[96,3072]{1,0:T(8,128)}) %reduce-scatter.15.cloned.1.call-update) | async-done | bytes 1179664 | tf_op jit(solution)/shard_map/while/body/eval_jaxpr/reduce_scatter | solution.py:120
  840.6 6.0 add_bitcast_fusion.3
  848.5 25.0 %all-reduce.45 = (bf16[768]{0:T(1024)(128)(2,1)S(1)}, bf16[768]{0:T(1024)(128)(2,1)S(1)}, bf16[768]{0:T(1024)(128)(2,1)S(1)}, bf16[768]{0:T(1024)(128)(2,1)S(1)}...) all-reduce(f32[768]{0:T(1024)S(1)} %get-tuple-element.1972, ...), channel_id=2, replica_groups=mesh['wide'=8,'narrow'=4] {'wide'}, use_global_device_ids=true, to_apply=%region_17.18.clone | all-reduce | flops 9984 | bytes 59904 | tf_op jit(solution)/shard_map/while
  876.7 12.0 all-reduce.46
  891.0 26.0 %all-reduce.50.cloned.1.call-done = (bf16[96,768]{1,0:T(8,128)(2,1)}, bf16[96,768]{1,0:T(8,128)(2,1)}, bf16[96,768]{1,0:T(8,128)(2,1)}, bf16[96,768]{1,0:T(8,128...) async-done(((bf16[96,768]{1,0:T(8,128)(2,1)}, bf16[96,768]{1,0:T(8,128)(2,1)}, bf16[96,768]{1,0:T(8,128)(2,1)}, bf16[96,768]{1,0:T(8,128)(2,1)}, ...) | async-done | bytes 1769488 | tf_op jit(solution)/shard_map/while/body/eval_jaxpr/psum | solution.py:128
  928.6 23.9 %all-reduce.44 = (bf16[768]{0:T(1024)(128)(2,1)S(1)}, bf16[768]{0:T(1024)(128)(2,1)S(1)}, bf16[768]{0:T(1024)(128)(2,1)S(1)}, bf16[768]{0:T(1024)(128)(2,1)S(1)}...) all-reduce(bf16[768]{0:T(1024)(128)(2,1)S(1)} %dynamic-update-slice, ...), channel_id=1, replica_groups=mesh['wide'=8,'narrow'=4] {'wide'}, use_global_device_ids=true, to_apply=%add.6 | all-reduce | flops 6912 | bytes 27648 | tf_op jit(solution)/shard_map/while
  956.1 7.9 all-gather.4
  1004.1 51.8 %while.109 = (s32[]{:T(128)}, f32[12,1024,64]{1,2,0:T(8,128)}, f32[12,1024]{1,0:T(8,128)S(1)}, bf16[12,1024,32]{2,1,0:T(8,128)(2,1)}, bf16[12,1024,32]{2,1,0:T(8...) while((s32[]{:T(128)}, f32[12,1024,64]{1,2,0:T(8,128)}, ...), condition=%wide.region_8.8_spmd.clone, body=%wide.region_6.7_spmd.clone.sunk | while | flops 211811328 | bytes 5273697 | solution.py:213
  1063.6 37.8 %multiply_convert_fusion.7 = (bf16[1024,3072]{1,0:T(8,128)(2,1)}, f32[1024,3072]{1,0:T(8,128)}, f32[1024,3072]{1,0:T(8,128)}) fusion(f32[3072]{0:T(1024)S(1)} %bitcast.491, s32[]{:T(128)S(6)} %select_n.289, bf16[768,3072]{1,0:T(8,128)(2,1)S(1)} %bitcast.494, f32[1024,768]{0,1:T(8,128)S(1)} %get-tuple-element.1939, ...), kind=kOutput, calls=%fused_computation.64.clone.1.clone | convolution fusion | flops 5052825600 | bytes 39348228 | tf_op jit(solution)/shard_map/while/body/eval_jaxpr/dot_general | solution.py:226
  1101.3 10.2 add_add_fusion.7
  1113.7 10.2 fusion.432
  1125.4 10.1 collective-permute-done
  1138.1 24.2 %collective-permute-done.1 = bf16[96,3072]{1,0:T(8,128)(2,1)S(1)} collective-permute-done((bf16[96,3072]{1,0:T(8,128)(2,1)S(1)}, bf16[96,3072]{1,0:T(8,128)(2,1)S(1)}, u32[]{:S(2)}, u32[]{:S(2)}) %collective-permute-start.1) | collective-permute-done | bytes 589856 | tf_op jit(solution)/shard_map/while/body/eval_jaxpr/ppermute | solution.py:23
  1165.0 14.9 collective-permute-done.2
  1185.8 13.7 collective-permute-done.3
  1211.1 18.5 %convert_reduce_fusion.24 = (f32[3072]{0:T(1024)S(1)}, bf16[1024,3072]{1,0:T(8,128)(2,1)}) fusion(f32[1024,3072]{1,0:T(8,128)} %get-tuple-element.1947, bf16[3072,768]{1,0:T(8,128)(2,1)} %all-gather.30.cloned.1.call-done, bf16[1,1024,768]{2,1,0:T(8,128)(2,1)S(1)} %constant_dynamic-slice_fusion.14, f32[1024,3072]{1,0:T(8,128)} %get-tuple-element.1949, ...), kind=kOutput, calls=%fused_computation.62.clone.1.clone | convolution fusion | flops 4885312512 | bytes 37773312 | tf_op jit(solution)/shard_map/while/body/eval_jaxpr/dot_general | solution.py:76
  1229.6 12.9 fusion.419
  1263.1 147.6 %while.110 = (s32[]{:T(128)}, f32[12,1024,32]{1,2,0:T(8,128)}, f32[12,1024,32]{1,2,0:T(8,128)}, bf16[12,1024,64]{1,2,0:T(8,128)(2,1)S(1)}, f32[12,1024,64]{2,1,0...) while((s32[]{:T(128)}, f32[12,1024,32]{1,2,0:T(8,128)}, ...), condition=%wide.region_15.16_spmd.clone, body=%wide.region_13.15_spmd.clone.sunk | while | flops 481888256 | bytes 10818697 | solution.py:261
  1442.7 10.6 fusion.431
  1482.2 32.9 %reduce-scatter.7.cloned.1.call-done = f32[96,768]{1,0:T(8,128)} async-done(((f32[768,768]{1,0:T(8,128)}), f32[96,768]{1,0:T(8,128)}) %reduce-scatter.7.cloned.1.call-update) | async-done | bytes 294928 | tf_op jit(solution)/shard_map/while/body/eval_jaxpr/reduce_scatter | solution.py:110
  1516.7 44.1 %reduce-scatter.13.cloned.1.call-done = f32[96,768]{1,0:T(8,128)} async-done(((f32[768,768]{1,0:T(8,128)}), f32[96,768]{1,0:T(8,128)}) %reduce-scatter.13.cloned.1.call-update) | async-done | bytes 294928 | tf_op jit(solution)/shard_map/while/body/eval_jaxpr/reduce_scatter | solution.py:116
  1562.4 44.1 %reduce-scatter.11.cloned.1.call-done = f32[96,768]{1,0:T(8,128)} async-done(((f32[768,768]{1,0:T(8,128)}), f32[96,768]{1,0:T(8,128)}) %reduce-scatter.11.cloned.1.call-update) | async-done | bytes 294928 | tf_op jit(solution)/shard_map/while/body/eval_jaxpr/reduce_scatter | solution.py:114
  1608.2 78.5 %reduce-scatter.15.cloned.1.call-done = f32[96,3072]{1,0:T(8,128)} async-done(((f32[768,3072]{1,0:T(8,128)}), f32[96,3072]{1,0:T(8,128)}) %reduce-scatter.15.cloned.1.call-update) | async-done | bytes 1179664 | tf_op jit(solution)/shard_map/while/body/eval_jaxpr/reduce_scatter | solution.py:120
  1696.8 24.9 %all-reduce.45 = (bf16[768]{0:T(1024)(128)(2,1)S(1)}, bf16[768]{0:T(1024)(128)(2,1)S(1)}, bf16[768]{0:T(1024)(128)(2,1)S(1)}, bf16[768]{0:T(1024)(128)(2,1)S(1)}...) all-reduce(f32[768]{0:T(1024)S(1)} %get-tuple-element.1972, ...), channel_id=2, replica_groups=mesh['wide'=8,'narrow'=4] {'wide'}, use_global_device_ids=true, to_apply=%region_17.18.clone | all-reduce | flops 9984 | bytes 59904 | tf_op jit(solution)/shard_map/while
  1725.0 12.0 all-reduce.46
  1739.3 26.1 %all-reduce.50.cloned.1.call-done = (bf16[96,768]{1,0:T(8,128)(2,1)}, bf16[96,768]{1,0:T(8,128)(2,1)}, bf16[96,768]{1,0:T(8,128)(2,1)}, bf16[96,768]{1,0:T(8,128...) async-done(((bf16[96,768]{1,0:T(8,128)(2,1)}, bf16[96,768]{1,0:T(8,128)(2,1)}, bf16[96,768]{1,0:T(8,128)(2,1)}, bf16[96,768]{1,0:T(8,128)(2,1)}, ...) | async-done | bytes 1769488 | tf_op jit(solution)/shard_map/while/body/eval_jaxpr/psum | solution.py:128
  (1114 shorter events, 782.5 us)
Async XLA Ops:
  33.0 17.1 collective-permute-start.12
  48.3 15.9 collective-permute-start.10
  68.3 45.8 %all-gather.18.cloned.1.call-start = ((), (), s32[]{:S(2)}) async-start(), calls=%async_computation.7 | async-start | bytes 1327104 | tf_op jit(solution)/shard_map/while/body/eval_jaxpr/all_gather | solution.py:89
  69.1 55.1 %all-gather.16.cloned.1.call-start = ((), (), s32[]{:S(2)}) async-start(), calls=%async_computation.6 | async-start | bytes 1327104 | tf_op jit(solution)/shard_map/while/body/eval_jaxpr/all_gather | solution.py:91
  69.8 80.2 %all-gather.20.cloned.1.call-start = ((), (), s32[]{:S(2)}) async-start(), calls=%async_computation.8 | async-start | bytes 1327104 | tf_op jit(solution)/shard_map/while/body/eval_jaxpr/all_gather | solution.py:93
  70.6 139.3 %all-gather.22.cloned.1.call-start = ((), (), s32[]{:S(2)}) async-start(), calls=%async_computation.9 | async-start | bytes 1327104 | tf_op jit(solution)/shard_map/while/body/eval_jaxpr/all_gather | solution.py:95
  71.1 182.1 %all-gather.24.cloned.1.call-start = ((), (), s32[]{:S(2)}) async-start(), calls=%async_computation.10 | async-start | bytes 5308416 | tf_op jit(solution)/shard_map/while/body/eval_jaxpr/all_gather | solution.py:101
  71.7 291.5 %all-gather.30.cloned.1.call-start = ((), (), s32[]{:S(2)}) async-start(), calls=%async_computation.13 | async-start | bytes 5308416 | tf_op jit(solution)/shard_map/while/body/eval_jaxpr/all_gather | solution.py:101
  263.5 140.9 %all-gather.28.cloned.1.call-start = ((), (), s32[]{:S(2)}) async-start(), calls=%async_computation.12 | async-start | bytes 1327104 | tf_op jit(solution)/shard_map/while/body/eval_jaxpr/all_gather | solution.py:95
  264.2 348.1 %reduce-scatter.17.cloned.1.call-start = ((), (), s32[]{:S(2)}) async-start(), calls=%async_computation.21 | async-start | bytes 10616832 | tf_op jit(solution)/shard_map/while/body/eval_jaxpr/reduce_scatter | solution.py:122
  276.0 338.5 %all-gather.34.cloned.1.call-start = ((), (), s32[]{:S(2)}) async-start(), calls=%async_computation.15 | async-start | bytes 1327104 | tf_op jit(solution)/shard_map/while/body/eval_jaxpr/all_gather | solution.py:91
  276.7 342.7 %all-gather.32.cloned.1.call-start = ((), (), s32[]{:S(2)}) async-start(), calls=%async_computation.14 | async-start | bytes 1327104 | tf_op jit(solution)/shard_map/while/body/eval_jaxpr/all_gather | solution.py:89
  277.4 346.9 %all-gather.26.cloned.1.call-start = ((), (), s32[]{:S(2)}) async-start(), calls=%async_computation.11 | async-start | bytes 1327104 | tf_op jit(solution)/shard_map/while/body/eval_jaxpr/all_gather | solution.py:93
  287.6 26.9 %collective-permute-start.1 = (bf16[96,3072]{1,0:T(8,128)(2,1)S(1)}, bf16[96,3072]{1,0:T(8,128)(2,1)S(1)}, u32[]{:S(2)}, u32[]{:S(2)}) collective-permute-start(bf16[96,3072]{1,0:T(8,128)(2,1)S(1)} %collective-permute-done), channel_id=1, source_target_pairs={{0,4},{4,8},{8,12},{12,16},{16,20},{20,24},{24,28},{28,0},{1,5},{5... | collective-permute-start | bytes 1769480 | tf_op jit(solution)/shard_map/while/body/eval_jaxpr/ppermute | solution.py:23
  287.6 26.9 %collective-permute-start.4 = (bf16[96,3072]{1,0:T(8,128)(2,1)S(1)}, bf16[96,3072]{1,0:T(8,128)(2,1)S(1)}, u32[]{:S(2)}, u32[]{:S(2)}) collective-permute-start(bf16[96,3072]{1,0:T(8,128)(2,1)S(1)} %copy-done.28), channel_id=1, source_target_pairs={{0,28},{4,0},{8,4},{12,8},{16,12},{20,16},{24,20},{28,24},{1,29},{... | collective-permute-start | bytes 1769480 | tf_op jit(solution)/shard_map/while/body/eval_jaxpr/ppermute | solution.py:25
  314.5 17.6 collective-permute-start.2
  315.3 19.9 %collective-permute-start.5 = (bf16[96,3072]{1,0:T(8,128)(2,1)S(1)}, bf16[96,3072]{1,0:T(8,128)(2,1)}, u32[]{:S(2)}, u32[]{:S(2)}) collective-permute-start(bf16[96,3072]{1,0:T(8,128)(2,1)S(1)} %collective-permute-done.4), channel_id=1, source_target_pairs={{0,28},{4,0},{8,4},{12,8},{16,12},{20,16},{24,20},{28,24},{1,29},{... | collective-permute-start | bytes 1769480 | tf_op jit(solution)/shard_map/while/body/eval_jaxpr/ppermute | solution.py:25
  332.1 19.6 %collective-permute-start.3 = (bf16[96,3072]{1,0:T(8,128)(2,1)}, bf16[96,3072]{1,0:T(8,128)(2,1)}, u32[]{:S(2)}, u32[]{:S(2)}) collective-permute-start(bf16[96,3072]{1,0:T(8,128)(2,1)} %collective-permute-done.2), channel_id=1, source_target_pairs={{0,4},{4,8},{8,12},{12,16},{16,20},{20,24},{24,28},{28,0},{1,5},{5... | collective-permute-start | bytes 1769480 | tf_op jit(solution)/shard_map/while/body/eval_jaxpr/ppermute | solution.py:23
  335.2 297.2 %reduce-scatter.9.cloned.1.call-start = ((), (), s32[]{:S(2)}) async-start(), calls=%async_computation.17 | async-start | bytes 2654208 | tf_op jit(solution)/shard_map/while/body/eval_jaxpr/reduce_scatter | solution.py:112
  335.2 27.1 %collective-permute-start.6 = (bf16[96,3072]{1,0:T(8,128)(2,1)}, bf16[96,3072]{1,0:T(8,128)(2,1)S(1)}, u32[]{:S(2)}, u32[]{:S(2)}) collective-permute-start(bf16[96,3072]{1,0:T(8,128)(2,1)} %collective-permute-done.5), channel_id=1, source_target_pairs={{0,28},{4,0},{8,4},{12,8},{16,12},{20,16},{24,20},{28,24},{1,29},{... | collective-permute-start | bytes 1769480 | tf_op jit(solution)/shard_map/while/body/eval_jaxpr/ppermute | solution.py:25
  579.8 87.2 %reduce-scatter.7.cloned.1.call-start = ((), (), s32[]{:S(2)}) async-start(), calls=%async_computation.16 | async-start | bytes 2654208 | tf_op jit(solution)/shard_map/while/body/eval_jaxpr/reduce_scatter | solution.py:110
  586.8 125.8 %reduce-scatter.13.cloned.1.call-start = ((), (), s32[]{:S(2)}) async-start(), calls=%async_computation.19 | async-start | bytes 2654208 | tf_op jit(solution)/shard_map/while/body/eval_jaxpr/reduce_scatter | solution.py:116
  591.8 166.4 %reduce-scatter.11.cloned.1.call-start = ((), (), s32[]{:S(2)}) async-start(), calls=%async_computation.18 | async-start | bytes 2654208 | tf_op jit(solution)/shard_map/while/body/eval_jaxpr/reduce_scatter | solution.py:114
  595.0 243.4 %reduce-scatter.15.cloned.1.call-start = ((), (), s32[]{:S(2)}) async-start(), calls=%async_computation.20 | async-start | bytes 10616832 | tf_op jit(solution)/shard_map/while/body/eval_jaxpr/reduce_scatter | solution.py:120
  605.6 311.3 %all-reduce.50.cloned.1.call-start = ((), (), s32[]{:S(2)}) async-start(), calls=%async_computation.22 | async-start | bytes 3538944 | tf_op jit(solution)/shard_map/while/body/eval_jaxpr/psum | solution.py:128
  921.5 43.1 %all-gather.18.cloned.1.call-start = ((), (), s32[]{:S(2)}) async-start(), calls=%async_computation.7 | async-start | bytes 1327104 | tf_op jit(solution)/shard_map/while/body/eval_jaxpr/all_gather | solution.py:89
  922.1 50.6 %all-gather.16.cloned.1.call-start = ((), (), s32[]{:S(2)}) async-start(), calls=%async_computation.6 | async-start | bytes 1327104 | tf_op jit(solution)/shard_map/while/body/eval_jaxpr/all_gather | solution.py:91
  922.9 75.6 %all-gather.20.cloned.1.call-start = ((), (), s32[]{:S(2)}) async-start(), calls=%async_computation.8 | async-start | bytes 1327104 | tf_op jit(solution)/shard_map/while/body/eval_jaxpr/all_gather | solution.py:93
  923.5 134.9 %all-gather.22.cloned.1.call-start = ((), (), s32[]{:S(2)}) async-start(), calls=%async_computation.9 | async-start | bytes 1327104 | tf_op jit(solution)/shard_map/while/body/eval_jaxpr/all_gather | solution.py:95
  924.2 177.1 %all-gather.24.cloned.1.call-start = ((), (), s32[]{:S(2)}) async-start(), calls=%async_computation.10 | async-start | bytes 5308416 | tf_op jit(solution)/shard_map/while/body/eval_jaxpr/all_gather | solution.py:101
  924.9 286.2 %all-gather.30.cloned.1.call-start = ((), (), s32[]{:S(2)}) async-start(), calls=%async_computation.13 | async-start | bytes 5308416 | tf_op jit(solution)/shard_map/while/body/eval_jaxpr/all_gather | solution.py:101
  1111.6 140.8 %all-gather.28.cloned.1.call-start = ((), (), s32[]{:S(2)}) async-start(), calls=%async_computation.12 | async-start | bytes 1327104 | tf_op jit(solution)/shard_map/while/body/eval_jaxpr/all_gather | solution.py:95
  1112.2 348.1 %reduce-scatter.17.cloned.1.call-start = ((), (), s32[]{:S(2)}) async-start(), calls=%async_computation.21 | async-start | bytes 10616832 | tf_op jit(solution)/shard_map/while/body/eval_jaxpr/reduce_scatter | solution.py:122
  1123.9 338.5 %all-gather.34.cloned.1.call-start = ((), (), s32[]{:S(2)}) async-start(), calls=%async_computation.15 | async-start | bytes 1327104 | tf_op jit(solution)/shard_map/while/body/eval_jaxpr/all_gather | solution.py:91
  1124.5 343.0 %all-gather.32.cloned.1.call-start = ((), (), s32[]{:S(2)}) async-start(), calls=%async_computation.14 | async-start | bytes 1327104 | tf_op jit(solution)/shard_map/while/body/eval_jaxpr/all_gather | solution.py:89
  1125.4 346.9 %all-gather.26.cloned.1.call-start = ((), (), s32[]{:S(2)}) async-start(), calls=%async_computation.11 | async-start | bytes 1327104 | tf_op jit(solution)/shard_map/while/body/eval_jaxpr/all_gather | solution.py:93
  1135.5 26.9 %collective-permute-start.1 = (bf16[96,3072]{1,0:T(8,128)(2,1)S(1)}, bf16[96,3072]{1,0:T(8,128)(2,1)S(1)}, u32[]{:S(2)}, u32[]{:S(2)}) collective-permute-start(bf16[96,3072]{1,0:T(8,128)(2,1)S(1)} %collective-permute-done), channel_id=1, source_target_pairs={{0,4},{4,8},{8,12},{12,16},{16,20},{20,24},{24,28},{28,0},{1,5},{5... | collective-permute-start | bytes 1769480 | tf_op jit(solution)/shard_map/while/body/eval_jaxpr/ppermute | solution.py:23
  1135.5 26.9 %collective-permute-start.4 = (bf16[96,3072]{1,0:T(8,128)(2,1)S(1)}, bf16[96,3072]{1,0:T(8,128)(2,1)S(1)}, u32[]{:S(2)}, u32[]{:S(2)}) collective-permute-start(bf16[96,3072]{1,0:T(8,128)(2,1)S(1)} %copy-done.28), channel_id=1, source_target_pairs={{0,28},{4,0},{8,4},{12,8},{16,12},{20,16},{24,20},{28,24},{1,29},{... | collective-permute-start | bytes 1769480 | tf_op jit(solution)/shard_map/while/body/eval_jaxpr/ppermute | solution.py:25
  1162.4 17.6 collective-permute-start.2
  1163.2 19.9 %collective-permute-start.5 = (bf16[96,3072]{1,0:T(8,128)(2,1)S(1)}, bf16[96,3072]{1,0:T(8,128)(2,1)}, u32[]{:S(2)}, u32[]{:S(2)}) collective-permute-start(bf16[96,3072]{1,0:T(8,128)(2,1)S(1)} %collective-permute-done.4), channel_id=1, source_target_pairs={{0,28},{4,0},{8,4},{12,8},{16,12},{20,16},{24,20},{28,24},{1,29},{... | collective-permute-start | bytes 1769480 | tf_op jit(solution)/shard_map/while/body/eval_jaxpr/ppermute | solution.py:25
  1180.0 19.6 %collective-permute-start.3 = (bf16[96,3072]{1,0:T(8,128)(2,1)}, bf16[96,3072]{1,0:T(8,128)(2,1)}, u32[]{:S(2)}, u32[]{:S(2)}) collective-permute-start(bf16[96,3072]{1,0:T(8,128)(2,1)} %collective-permute-done.2), channel_id=1, source_target_pairs={{0,4},{4,8},{8,12},{12,16},{16,20},{20,24},{24,28},{28,0},{1,5},{5... | collective-permute-start | bytes 1769480 | tf_op jit(solution)/shard_map/while/body/eval_jaxpr/ppermute | solution.py:23
  1183.1 297.3 %reduce-scatter.9.cloned.1.call-start = ((), (), s32[]{:S(2)}) async-start(), calls=%async_computation.17 | async-start | bytes 2654208 | tf_op jit(solution)/shard_map/while/body/eval_jaxpr/reduce_scatter | solution.py:112
  1183.1 27.2 %collective-permute-start.6 = (bf16[96,3072]{1,0:T(8,128)(2,1)}, bf16[96,3072]{1,0:T(8,128)(2,1)S(1)}, u32[]{:S(2)}, u32[]{:S(2)}) collective-permute-start(bf16[96,3072]{1,0:T(8,128)(2,1)} %collective-permute-done.5), channel_id=1, source_target_pairs={{0,28},{4,0},{8,4},{12,8},{16,12},{20,16},{24,20},{28,24},{1,29},{... | collective-permute-start | bytes 1769480 | tf_op jit(solution)/shard_map/while/body/eval_jaxpr/ppermute | solution.py:25
  1427.7 87.3 %reduce-scatter.7.cloned.1.call-start = ((), (), s32[]{:S(2)}) async-start(), calls=%async_computation.16 | async-start | bytes 2654208 | tf_op jit(solution)/shard_map/while/body/eval_jaxpr/reduce_scatter | solution.py:110
  1434.5 126.3 %reduce-scatter.13.cloned.1.call-start = ((), (), s32[]{:S(2)}) async-start(), calls=%async_computation.19 | async-start | bytes 2654208 | tf_op jit(solution)/shard_map/while/body/eval_jaxpr/reduce_scatter | solution.py:116
  1439.5 167.0 %reduce-scatter.11.cloned.1.call-start = ((), (), s32[]{:S(2)}) async-start(), calls=%async_computation.18 | async-start | bytes 2654208 | tf_op jit(solution)/shard_map/while/body/eval_jaxpr/reduce_scatter | solution.py:114
  1442.6 244.1 %reduce-scatter.15.cloned.1.call-start = ((), (), s32[]{:S(2)}) async-start(), calls=%async_computation.20 | async-start | bytes 10616832 | tf_op jit(solution)/shard_map/while/body/eval_jaxpr/reduce_scatter | solution.py:120
  1453.3 312.1 %all-reduce.50.cloned.1.call-start = ((), (), s32[]{:S(2)}) async-start(), calls=%async_computation.22 | async-start | bytes 3538944 | tf_op jit(solution)/shard_map/while/body/eval_jaxpr/psum | solution.py:128
  (211 other events, 3227.1 us)
Sparse Core Ops, SparseCore 0:
  71.0 27.1 all-gather.17
  100.2 24.0 all-gather.15
  126.1 23.9 all-gather.19
  151.8 23.9 all-gather.21
  177.5 38.7 all-gather.23
  263.6 48.6 all-gather.29
  314.2 29.5 all-gather.27
  347.2 76.8 reduce-scatter.16
  426.0 23.9 all-gather.33
  451.7 23.9 all-gather.31
  477.5 23.9 all-gather.25
  580.0 41.3 reduce-scatter.8
  624.7 42.3 reduce-scatter.6
  670.3 42.3 reduce-scatter.12
  715.8 42.3 reduce-scatter.10
  761.6 76.8 reduce-scatter.14
  841.1 75.7 all-reduce.49
  923.9 22.8 all-gather.17
  948.7 24.0 all-gather.15
  974.5 23.9 all-gather.19
  1000.3 23.9 all-gather.21
  1026.2 38.7 all-gather.23
  1111.7 48.7 all-gather.29
  1162.2 29.2 all-gather.27
  1195.0 76.8 reduce-scatter.16
  1273.6 23.9 all-gather.33
  1299.3 23.9 all-gather.31
  1325.2 23.8 all-gather.25
  1427.9 41.5 reduce-scatter.8
  1472.7 42.3 reduce-scatter.6
  1518.4 42.3 reduce-scatter.12
  1564.1 42.3 reduce-scatter.10
  1609.9 76.8 reduce-scatter.14
  1689.6 75.7 all-reduce.49
